TPU v7x, 16 devices: a whole 2x2x2 slice. The times are simulated.
16 devices in a mesh: ep: 16 (over z, y, x, core).
Axes of the slice: x: 2, y: 2, z: 2, core: 2. Of those that a mesh axis runs over, the one named last changes fastest.
Arguments:
- hidden: bfloat16 [32768, 768], P('ep')
- w_router: float32 [768, 32], replicated
- expert_ids: int32 [32768, 2], P('ep')
- w_one: bfloat16 [32, 768, 3072], P('ep')
- w_three: bfloat16 [32, 768, 3072], P('ep')
- w_two: bfloat16 [32, 3072, 768], P('ep')
Outputs:
- output: bfloat16 [32768, 768], P('ep')
All inputs are finite; a program needn't handle non-finite values.
Results may differ from a plain program's by a relative error of at most 0.0086898.
Values are sent between devices in bfloat16 or wider.
A program may use at most 1 GiB of HBM per device.

v0:
```python
import functools

import jax
import jax.numpy as jnp
from jax import lax
from jax.experimental import pallas as pl
from jax.experimental.pallas import tpu as pltpu
from jax.sharding import PartitionSpec as P


F32 = jnp.float32
BF16 = jnp.bfloat16
I32 = jnp.int32
TILE = 16
CHUNKS = ((0, 256), (256, 256))
VMEM_BYTES = 60 * 1024 * 1024


def _dot(a, b):
    return jnp.dot(a, b, preferred_element_type=F32)


def route_slots(local_count, row_cap, n_exp, ids_ref, slot_ref, cnt_ref):
    tok = ids_ref.shape[1]
    ids = ids_ref[...]
    id_a, id_b = ids[0:1], ids[1:2]
    row = lax.broadcasted_iota(I32, (n_exp, tok), 0)
    oh_a, oh_b = row == id_a, row == id_b
    zero = jnp.zeros((), F32)
    chosen = jnp.where(oh_a | oh_b, 1.0, 0.0).astype(F32)
    width = 256
    tri = lax.broadcasted_iota(I32, (width, width), 0) < lax.broadcasted_iota(I32, (width, width), 1)
    tri = jnp.where(tri, 1.0, 0.0).astype(BF16)
    before = jnp.zeros((n_exp, 1), F32)
    ranks = []
    for k in range(tok // width):
        blk = chosen[:, k * width : (k + 1) * width]
        ranks.append(_dot(blk.astype(BF16), tri) + before)
        before = before + jnp.sum(blk, axis=1, keepdims=True)
    rank = jnp.concatenate(ranks, axis=1)
    cnt_ref[...] = jnp.broadcast_to(before, cnt_ref.shape).astype(I32)

    def slot_of(ident, onehot):
        here = jnp.sum(jnp.where(onehot, rank, zero), axis=0, keepdims=True)
        dev = ident // local_count
        lower = (row < ident) & (row >= dev * local_count)
        base = jnp.sum(jnp.where(lower, jnp.broadcast_to(before, (n_exp, tok)), zero), axis=0, keepdims=True)
        return dev.astype(F32) * row_cap + here + base

    s_a, s_b = slot_of(id_a, oh_a), slot_of(id_b, oh_b)
    slot_ref[...] = jnp.concatenate([s_a, s_b] * 4, axis=0).astype(I32)


def route_gates(x_ref, wr_ref, ids_ref, slot_ref, cols_ref):
    tok = x_ref.shape[0]
    n_exp = wr_ref.shape[0]
    w = wr_ref[...]
    w_hi = w.astype(BF16)
    rest = w - w_hi.astype(F32)
    w_mid = rest.astype(BF16)
    w_lo = (rest - w_mid.astype(F32)).astype(BF16)
    nt = (((1,), (1,)), ((), ()))
    w_all = jnp.concatenate([w_hi, w_mid, w_lo], axis=0)
    parts = lax.dot_general(w_all, x_ref[...], nt, preferred_element_type=F32)
    logits = parts[:n_exp] + (parts[n_exp : 2 * n_exp] + parts[2 * n_exp :])
    ids = ids_ref[...]
    row = lax.broadcasted_iota(I32, (n_exp, tok), 0)
    zero = jnp.zeros((), F32)
    l_a = jnp.sum(jnp.where(row == ids[0:1], logits, zero), axis=0, keepdims=True)
    l_b = jnp.sum(jnp.where(row == ids[1:2], logits, zero), axis=0, keepdims=True)
    top = jnp.maximum(l_a, l_b)
    e_a, e_b = jnp.exp(l_a - top), jnp.exp(l_b - top)
    g_a, g_b = e_a / (e_a + e_b), e_b / (e_a + e_b)
    slots = slot_ref[0:2, :].astype(F32)
    cols_ref[...] = jnp.concatenate([slots, g_a, g_b, slots, g_a, g_b], axis=0).T


WIDE = 512
GROUP = 16
STEP = GROUP * TILE


MESH = pl.DeviceIdType.MESH


def partner(me, offset):
    other = me
    for bit in (1, 2, 4, 8):
        other = other + ((offset // bit) % 2) * (bit - 2 * bit * ((me // bit) % 2))
    return other


def pair_of(p):
    j, r = (p - 1) // 2, (p - 1) % 2
    near = 8 - 4 * j + 2 * (j // 2)
    return 14 - near + r, near + r


def ship_kernel(row_cap, n_dev, chunks, local, ids_ref, wr_ref, x_ref, got_ref, next_ref, all_ref, cols_ref, slot_ref, cnt_ref, sbuf, vbuf, send_sems, recv_sems, own_sem, next_sems, cs_sems, cr_sems, co_sem):
    me = lax.axis_index("ep")
    tok = x_ref.shape[0]
    (start, size), (start1, size1) = chunks

    def pack(dev, first, rows):
        want = lax.broadcasted_iota(I32, (rows, tok), 0) + (dev * row_cap + first)
        hit = (want == slot_ref[0:1, :]) | (want == slot_ref[1:2, :])
        pick = jnp.where(hit, 1.0, 0.0).astype(BF16)
        return _dot(pick, x_ref[...]).astype(BF16)

    def send(k):
        return pltpu.make_async_remote_copy(
            src_ref=sbuf.at[k],
            dst_ref=got_ref.at[me],
            send_sem=send_sems.at[k],
            recv_sem=recv_sems.at[k],
            device_id=(partner(me, k),),
            device_id_type=MESH,
        )

    def tell(k):
        return pltpu.make_async_remote_copy(
            src_ref=cnt_ref,
            dst_ref=all_ref.at[me],
            send_sem=cs_sems.at[k],
            recv_sem=cr_sems.at[k],
            device_id=(partner(me, k),),
            device_id_type=MESH,
        )

    own_counts = pltpu.make_async_copy(cnt_ref, all_ref.at[me], co_sem)

    def keep(d):
        return pltpu.make_async_copy(vbuf.at[d], next_ref.at[d], next_sems.at[d])

    def pack_first(k0, k1):
        @pl.loop(0, 2)
        def _(r):
            k = k0 + r * (k1 - k0)
            sbuf[k] = pack(partner(me, k), start, size)

    barrier = pltpu.get_barrier_semaphore()
    for k in range(1, n_dev):
        pl.semaphore_signal(barrier, inc=1, device_id=(partner(me, k),), device_id_type=MESH)
    route_slots(local, row_cap, wr_ref.shape[0], ids_ref, slot_ref, cnt_ref)
    pack_first(14, 15)
    pl.semaphore_wait(barrier, n_dev - 1)
    send(14).start()
    send(15).start()
    own_counts.start()

    @pl.loop(1, n_dev)
    def _(k):
        tell(k).start()

    pack_first(6, 8)

    @pl.loop(1, 7)
    def _(p):
        k0, k1 = pair_of(p)

        @pl.when(p <= 2)
        def _():
            send(13 + p).wait_send()

        @pl.when(p >= 3)
        def _():
            for k in pair_of(p - 2):
                send(k).wait_send()

        send(k0).start()
        send(k1).start()

        @pl.when(p < 6)
        def _():
            pack_first(*pair_of(p + 1))

        @pl.loop((n_dev * (p - 1)) // 6, (n_dev * p) // 6)
        def _(d):
            vbuf[d] = pack(d, start1, size1)

            @pl.when(d > 0)
            def _():
                keep(d - 1).start()

    pack_first(0, 1)
    keep(n_dev - 1).start()
    route_gates(x_ref, wr_ref, ids_ref, slot_ref, cols_ref)
    send(1).start()
    own = pltpu.make_async_copy(sbuf.at[0], got_ref.at[me], own_sem)
    own.start()
    for p in (5, 6):
        for k in pair_of(p):
            send(k).wait_send()
    send(1).wait_send()
    own.wait()
    own_counts.wait()

    @pl.loop(0, n_dev)
    def _(d):
        keep(d).wait()

    @pl.loop(1, n_dev)
    def _(k):
        tell(k).wait_send()
        tell(k).wait_recv()
        send(k).wait_recv()


def ffn_kernel(start, size, n_src, bound_ref, x_hbm, w1_hbm, w3_hbm, w2_hbm, out_ref, x_ref, w1, w3, w2, xbuf, hbuf, list_ref, low_ref, high_ref, used_ref, sems, x_sems):
    n_loc, _, ff = w1.shape
    n_f = ff // WIDE
    per = size // TILE

    def copy(e, which, f):
        cut = pl.ds(f * WIDE, WIDE)
        at = (e, cut) if which == 2 else (e, slice(None), cut)
        src, dst = ((w1_hbm, w1), (w3_hbm, w3), (w2_hbm, w2))[which]
        return pltpu.make_async_copy(src.at[at], dst.at[at], sems.at[e, which, f])

    quarter = x_ref.shape[0] // 4

    def row_copy(q):
        at = pl.ds(q * quarter, quarter)
        return pltpu.make_async_copy(x_hbm.at[at], x_ref.at[at], x_sems.at[q])

    for q in range(4):
        row_copy(q).start()

    @pl.loop(0, n_loc)
    def _(e):
        def need(s, any_):
            lo, hi = bound_ref[e, s], bound_ref[e + 1, s]
            return any_ | ((lo < start + size) & (hi > start) & (hi > lo)).astype(I32)

        used = lax.fori_loop(0, n_src, need, jnp.int32(0))
        used_ref[e] = used

        @pl.when(used > 0)
        def _():
            @pl.loop(0, n_f)
            def _(f):
                copy(e, 0, f).start()
                copy(e, 1, f).start()

            @pl.loop(0, n_f)
            def _(f):
                copy(e, 2, f).start()

    out_ref[...] = jnp.zeros_like(out_ref)
    for q in range(4):
        row_copy(q).wait()

    @pl.loop(0, n_loc)
    def _(e):
        @pl.when(used_ref[e] > 0)
        def _():
            def collect(s, cnt):
                lo = jnp.clip(bound_ref[e, s] - start, 0, size)
                hi = jnp.clip(bound_ref[e + 1, s] - start, 0, size)
                t_lo = lo // TILE
                t_hi = jnp.where(hi > lo, (hi + TILE - 1) // TILE, t_lo)

                def add(t, k):
                    list_ref[k] = s * per + t
                    low_ref[k] = lo - t * TILE
                    high_ref[k] = hi - t * TILE
                    return k + 1

                return lax.fori_loop(t_lo, t_hi, add, cnt)

            cnt = lax.fori_loop(0, n_src, collect, jnp.int32(0))
            groups = (cnt + GROUP - 1) // GROUP

            @pl.loop(cnt, groups * GROUP)
            def _(k):
                list_ref[k] = 0
                low_ref[k] = 0
                high_ref[k] = 0

            def tile_of(g, j):
                return pl.ds(pl.multiple_of(list_ref[g * GROUP + j] * TILE, TILE), TILE)

            def columns(f):
                cut = pl.ds(f * WIDE if isinstance(f, int) else pl.multiple_of(f * WIDE, WIDE), WIDE)
                xb = xbuf[...]
                u = _dot(xb, w1[e, :, cut])
                v = _dot(xb, w3[e, :, cut])
                hbuf[:, cut] = (u * jax.nn.sigmoid(u) * v).astype(BF16)

            @pl.loop(0, groups)
            def _(g):
                for j in range(GROUP):
                    xbuf[j * TILE : (j + 1) * TILE, :] = x_ref[tile_of(g, j), :]

                @pl.when(g == 0)
                def _():
                    @pl.loop(0, n_f)
                    def _(f):
                        copy(e, 0, f).wait()
                        copy(e, 1, f).wait()
                        columns(f)

                    @pl.loop(0, n_f)
                    def _(f):
                        copy(e, 2, f).wait()

                @pl.when(g > 0)
                def _():
                    for f in range(n_f):
                        columns(f)

                y = _dot(hbuf[...], w2[e]).astype(BF16)
                row = lax.broadcasted_iota(I32, (TILE, 1), 0)
                for j in range(GROUP):
                    own = (row >= low_ref[g * GROUP + j]) & (row < high_ref[g * GROUP + j])
                    at = tile_of(g, j)
                    out_ref[at, :] = jnp.where(own, y[j * TILE : (j + 1) * TILE], out_ref[at, :])


def gated(cols, ids, rows):
    add = 0.0
    for k in range(2):
        pick = jnp.where(ids == cols[:, k : k + 1], 1.0, 0.0).astype(BF16)
        add = add + cols[:, 2 + k : 3 + k] * _dot(pick, rows)
    return add


def bring_kernel(row_cap, n_dev, chunks, made_ref, back_hbm, cols_ref, out_ref, back, got, acc, rows_ref, send_sems, recv_sems, own_sem, back_sems):
    me = lax.axis_index("ep")
    (start, size), (start1, size1) = chunks
    tok = cols_ref.shape[0]
    block = 512

    def send(k):
        return pltpu.make_async_remote_copy(
            src_ref=made_ref.at[partner(me, k)],
            dst_ref=got.at[me],
            send_sem=send_sems.at[k],
            recv_sem=recv_sems.at[k],
            device_id=(partner(me, k),),
            device_id_type=MESH,
        )

    def fetch(g):
        at = pl.ds(pl.multiple_of(g * 2 * size, 2 * size), 2 * size)
        return pltpu.make_async_copy(back_hbm.at[at], back.at[at], back_sems.at[g])

    barrier = pltpu.get_barrier_semaphore()
    for k in range(1, n_dev):
        pl.semaphore_signal(barrier, inc=1, device_id=(partner(me, k),), device_id_type=MESH)
    groups = n_dev // 2

    @pl.loop(0, groups)
    def _(g):
        fetch(g).start()

    acc[...] = jnp.zeros_like(acc)
    pl.semaphore_wait(barrier, n_dev - 1)
    send(14).start()
    send(15).start()
    send(1).start()
    own = pltpu.make_async_copy(made_ref.at[me], got.at[me], own_sem)
    own.start()
    lane = lax.broadcasted_iota(I32, (1, 2 * size), 1)

    @pl.loop(1, 9)
    def _(p):
        @pl.when(p <= 2)
        def _():
            send(13 + p).wait_send()

        @pl.when(p >= 3)
        def _():
            for k in pair_of(p - 2):
                send(k).wait_send()

        @pl.when(p <= 6)
        def _():
            for k in pair_of(p):
                send(k).start()

        low = jnp.minimum((groups * (p - 1)) // 6, groups)
        high = jnp.minimum((groups * p) // 6, groups)
        near, far = pair_of(p - 2)
        k0 = jnp.where(p == 1, 0, jnp.where(p == 2, 14, near))
        k1 = jnp.where(p == 1, 1, jnp.where(p == 2, 15, far))
        d0, d1 = partner(me, k0), partner(me, k1)

        @pl.loop(low, high + 1)
        def _(g):
            @pl.when(g < high)
            def _():
                fetch(g).wait()
                rows_ref[...] = back[pl.ds(pl.multiple_of(g * 2 * size, 2 * size), 2 * size), :]

            @pl.when(g == high)
            def _():
                @pl.when(p == 1)
                def _():
                    own.wait()

                @pl.when(p > 1)
                def _():
                    send(k0).wait_recv()

                send(k1).wait_recv()
                rows_ref[:size1, :] = got[d0]
                rows_ref[size1:, :] = got[d1]

            at0 = jnp.where(g < high, 2 * g * row_cap + start, d0 * row_cap + start1)
            at1 = jnp.where(g < high, (2 * g + 1) * row_cap + start, d1 * row_cap + start1)
            ids = jnp.where(lane < size, at0 + lane, at1 + lane - size).astype(F32)
            rows = rows_ref[...]
            for t in range(tok // block):
                at = slice(t * block, (t + 1) * block)
                acc[at, :] += gated(cols_ref[at, :], ids, rows)

    out_ref[...] = acc[...].astype(BF16)
    send(1).wait_send()


def _params(vmem_limit_bytes=VMEM_BYTES):
    return pltpu.CompilerParams(vmem_limit_bytes=vmem_limit_bytes)


def solution(mesh):
    n = mesh.shape["ep"]

    def body(x, w_router, ids, w1, w3, w2):
        tok, dim = x.shape
        local = w1.shape[0]
        ff = w1.shape[2]
        n_exp = n * local
        cap = 4 * tok // n
        smem = pl.BlockSpec(memory_space=pltpu.SMEM)
        vmem = pl.BlockSpec(memory_space=pltpu.VMEM)
        hbm = pl.BlockSpec(memory_space=pl.ANY)
        ship = pl.pallas_call(
            functools.partial(ship_kernel, cap, n, CHUNKS, local),
            in_specs=[vmem, vmem, vmem],
            out_specs=[hbm, hbm, hbm, vmem],
            out_shape=[jax.ShapeDtypeStruct((n, size, dim), BF16) for _, size in CHUNKS]
            + [jax.ShapeDtypeStruct((n, n_exp, 128), I32), jax.ShapeDtypeStruct((tok, 8), F32)],
            scratch_shapes=[
                pltpu.VMEM((8, tok), I32),
                pltpu.VMEM((n_exp, 128), I32),
                pltpu.VMEM((n, CHUNKS[0][1], dim), BF16),
                pltpu.VMEM((n, CHUNKS[1][1], dim), BF16),
                pltpu.SemaphoreType.DMA((n,)),
                pltpu.SemaphoreType.DMA((n,)),
                pltpu.SemaphoreType.DMA,
                pltpu.SemaphoreType.DMA((n,)),
                pltpu.SemaphoreType.DMA((n,)),
                pltpu.SemaphoreType.DMA((n,)),
                pltpu.SemaphoreType.DMA,
            ],
            compiler_params=pltpu.CompilerParams(
                vmem_limit_bytes=VMEM_BYTES, collective_id=0, has_side_effects=True
            ),
            cost_estimate=pl.CostEstimate(flops=10**11, bytes_accessed=1, transcendentals=0),
            name="ship",
        )
        first_rows, second_rows, every, cols = ship(ids.T, w_router.T, x)
        at = lax.axis_index("ep") * local
        per_exp = lax.dynamic_slice(every, (0, at, 0), (n, local, 1))[:, :, 0]
        ends = jnp.cumsum(per_exp, axis=1).T
        bounds = jnp.concatenate([jnp.zeros((1, n), I32), ends], axis=0)
        for index, (start, size) in enumerate(CHUNKS):
            if index == 0:
                got = first_rows
            else:
                got = lax.all_to_all(second_rows, "ep", 0, 0, tiled=True)
            rows = n * size
            made = pl.pallas_call(
                functools.partial(ffn_kernel, start, size, n),
                in_specs=[smem, hbm, hbm, hbm, hbm],
                out_specs=vmem,
                scratch_shapes=[
                    pltpu.VMEM((rows, dim), BF16),
                    pltpu.VMEM((local, dim, ff), BF16),
                    pltpu.VMEM((local, dim, ff), BF16),
                    pltpu.VMEM((local, ff, dim), BF16),
                    pltpu.VMEM((STEP, dim), BF16),
                    pltpu.VMEM((STEP, ff), BF16),
                    pltpu.SMEM((rows // TILE + GROUP,), I32),
                    pltpu.SMEM((rows // TILE + GROUP,), I32),
                    pltpu.SMEM((rows // TILE + GROUP,), I32),
                    pltpu.SMEM((local,), I32),
                    pltpu.SemaphoreType.DMA((local, 3, ff // WIDE)),
                    pltpu.SemaphoreType.DMA((4,)),
                ],
                out_shape=jax.ShapeDtypeStruct((rows, dim), BF16),
                compiler_params=_params(),
                cost_estimate=pl.CostEstimate(flops=6 * rows * dim * ff, bytes_accessed=1, transcendentals=0),
            )
            made = made(bounds, got.reshape(rows, dim), w1, w3, w2)
            if index == 0:
                back = lax.all_to_all(made.reshape(n, size, dim), "ep", 0, 0, tiled=True)
        return pl.pallas_call(
            functools.partial(bring_kernel, cap, n, CHUNKS),
            in_specs=[hbm, hbm, vmem],
            out_specs=vmem,
            out_shape=jax.ShapeDtypeStruct((tok, dim), BF16),
            scratch_shapes=[
                pltpu.VMEM((n * CHUNKS[0][1], dim), BF16),
                pltpu.VMEM((n, CHUNKS[1][1], dim), BF16),
                pltpu.VMEM((tok, dim), F32),
                pltpu.VMEM((2 * CHUNKS[0][1], dim), BF16),
                pltpu.SemaphoreType.DMA((n,)),
                pltpu.SemaphoreType.DMA((n,)),
                pltpu.SemaphoreType.DMA,
                pltpu.SemaphoreType.DMA((n // 2,)),
            ],
            compiler_params=pltpu.CompilerParams(
                vmem_limit_bytes=VMEM_BYTES, collective_id=1, has_side_effects=True
            ),
            cost_estimate=pl.CostEstimate(flops=10**11, bytes_accessed=1, transcendentals=0),
            name="bring",
        )(made.reshape(n, CHUNKS[1][1], dim), back.reshape(n * CHUNKS[0][1], dim), cols)

    return jax.shard_map(
        body,
        mesh=mesh,
        in_specs=(P("ep", None), P(None, None), P("ep", None), P("ep", None, None), P("ep", None, None), P("ep", None, None)),
        out_specs=P("ep", None),
        check_vma=False,
    )
```

profile of v0, /device:TPU:11, one launch (start us, length us, event | category | flops | bytes accessed | tf_op | source)
XLA Modules:
  0.0 341.1 jit_solution(265036375025707001)
XLA Ops:
  0.0 79.5 %ship.1 = (bf16[16,256,768]{2,1,0:T(8,128)(2,1)}, bf16[16,256,768]{2,1,0:T(8,128)(2,1)}, s32[16,32,128]{2,1,0:T(8,128)}, f32[2048,8]{1,0:T(8,128)}) custom-call(s32[2,2048]{1,0:T(2,128)} %bitcast.13, f32[32,768]{1,0:T(8,128)} %bitcast.12, bf16[2048,768]{1,0:T(8,128)(2,1)} %x_ref.1), custom_call_target="tpu_custom_call" | custom-call | flops 99999997952 | bytes 1 | tf_op jit(solution)/shard_map/ship/pallas_call | solution.py:463
  79.5 9.6 %all-to-all-start = ((bf16[16,256,768]{2,1,0:T(8,128)(2,1)}), bf16[16,256,768]{2,1,0:T(8,128)(2,1)}, u32[]{:S(2)}, u32[]{:S(2)}) async-start(bf16[16,256,768]{2,1,0:T(8,128)(2,1)} %get-tuple-element.10), calls=%async_computation | async-start | bytes 12582912 | tf_op jit(solution)/shard_map/all_to_all | solution.py:472
  89.2 0.8 constant_dynamic-slice_fusion
  90.0 0.1 copy.7
  90.1 0.6 concatenate.3.bound_ref
  90.7 79.3 %shard_map.65 = bf16[4096,768]{1,0:T(8,128)(2,1)} custom-call(s32[3,16]{1,0:T(4,128)} %concatenate.3.bound_ref, bf16[4096,768]{1,0:T(8,128)(2,1)} %bitcast.14, bf16[2,768,3072]{2,1,0:T(8,128)(2,1)} %w1_hbm.3, bf16[2,768,3072]{2,1,0:T(8,128)(2,1)} %w3_hbm.3, bf16[2,3072,768]{2,1,0:T(8,128)(2,1)} %w2_hbm.3), custom_call_target="tpu_custom_call" | custom-call | flops 57982058496 | bytes 1 | tf_op jit(solution)/shard_map/pallas_call | solution.py:496
  170.0 0.0 all-to-all-done
  170.0 3.5 %all-to-all-start.1 = ((bf16[16,256,768]{2,1,0:T(8,128)(2,1)}), bf16[16,256,768]{2,1,0:T(8,128)(2,1)}, u32[]{:S(2)}, u32[]{:S(2)}) async-start(bf16[16,256,768]{2,1,0:T(8,128)(2,1)} %bitcast.9), calls=%async_computation.1 | async-start | bytes 12582912 | tf_op jit(solution)/shard_map/all_to_all | solution.py:498
  173.5 81.0 %shard_map.64 = bf16[4096,768]{1,0:T(8,128)(2,1)} custom-call(s32[3,16]{1,0:T(4,128)} %concatenate.3.bound_ref, bf16[4096,768]{1,0:T(8,128)(2,1)} %bitcast.4.x_hbm, bf16[2,768,3072]{2,1,0:T(8,128)(2,1)} %w1_hbm.3, bf16[2,768,3072]{2,1,0:T(8,128)(2,1)} %w3_hbm.3, bf16[2,3072,768]{2,1,0:T(8,128)(2,1)} %w2_hbm.3), custom_call_target="tpu_custom_call" | custom-call | flops 57982058496 | bytes 1 | tf_op jit(solution)/shard_map/pallas_call | solution.py:496
  254.6 0.0 all-to-all-done.1
  254.6 82.7 %bring.1 = bf16[2048,768]{1,0:T(8,128)(2,1)} custom-call(bf16[16,256,768]{2,1,0:T(8,128)(2,1)} %bitcast.15, bf16[4096,768]{1,0:T(8,128)(2,1)} %bitcast.8.back_hbm, f32[2048,8]{1,0:T(8,128)} %get-tuple-element.12.cols_ref), custom_call_target="tpu_custom_call" | custom-call | flops 99999997952 | bytes 1 | tf_op jit(solution)/shard_map/bring/pallas_call | solution.py:499
  337.3 3.8 %copy.9 = bf16[2048,768]{1,0:T(8,128)(2,1)} copy(bf16[2048,768]{1,0:T(8,128)(2,1)} %bring.1) | data formatting | bytes 6291456
  (1 shorter events, 0.0 us)
Async XLA Ops:
  79.5 90.5 %all-to-all-start = ((bf16[16,256,768]{2,1,0:T(8,128)(2,1)}), bf16[16,256,768]{2,1,0:T(8,128)(2,1)}, u32[]{:S(2)}, u32[]{:S(2)}) async-start(bf16[16,256,768]{2,1,0:T(8,128)(2,1)} %get-tuple-element.10), calls=%async_computation | async-start | bytes 12582912 | tf_op jit(solution)/shard_map/all_to_all | solution.py:472
  170.0 84.5 %all-to-all-start.1 = ((bf16[16,256,768]{2,1,0:T(8,128)(2,1)}), bf16[16,256,768]{2,1,0:T(8,128)(2,1)}, u32[]{:S(2)}, u32[]{:S(2)}) async-start(bf16[16,256,768]{2,1,0:T(8,128)(2,1)} %bitcast.9), calls=%async_computation.1 | async-start | bytes 12582912 | tf_op jit(solution)/shard_map/all_to_all | solution.py:498
where the time goes:
time: 344 us; the launch traced here: 341 us
  Pallas kernels  323 us (94%)
  starting transfers between devices  13.1 us (4%)
  local copies, waits for them, and re-layouts  5.29 us (2%)
    pallas_call x2, Pallas kernels, body(): made = made(bounds, got.reshape(rows, dim), w1, w3, w2)  160 us
    pallas_call x1, Pallas kernels, body(): pl.pallas_call(functools.partial(bring_kernel, cap, n, CHUNKS), in_specs=...  82.7 us
    pallas_call x1, Pallas kernels, body(): first_rows, second_rows, every, cols = ship(ids.T, w_router.T, x)  79.5 us
    all_to_all x1, starting transfers between devices, body(): got = lax.all_to_all(second_rows, 'ep', 0, 0, tiled=True)  9.64 us
  transfers between devices with their start and end apart: 2, of which 0 were waited for; matrix products, arithmetic and copies ran while one was open for 0% of the time, Pallas kernels for 47%

commit v1 on v0

--- a/solution.py
+++ b/solution.py
@@ -96,7 +96,7 @@
     return 14 - near + r, near + r
 
 
-def ship_kernel(row_cap, n_dev, chunks, local, ids_ref, wr_ref, x_ref, got_ref, next_ref, all_ref, cols_ref, slot_ref, cnt_ref, sbuf, vbuf, send_sems, recv_sems, own_sem, next_sems, cs_sems, cr_sems, co_sem):
+def ship_kernel(row_cap, n_dev, chunks, slot_ref, cnt_ref, ids_ref, wr_ref, x_ref, got_ref, next_ref, all_ref, cols_ref, sbuf, vbuf, send_sems, recv_sems, own_sem, next_sems, cs_sems, cr_sems, co_sem):
     me = lax.axis_index("ep")
     tok = x_ref.shape[0]
     (start, size), (start1, size1) = chunks
@@ -141,7 +141,6 @@
     barrier = pltpu.get_barrier_semaphore()
     for k in range(1, n_dev):
         pl.semaphore_signal(barrier, inc=1, device_id=(partner(me, k),), device_id_type=MESH)
-    route_slots(local, row_cap, wr_ref.shape[0], ids_ref, slot_ref, cnt_ref)
     pack_first(14, 15)
     pl.semaphore_wait(barrier, n_dev - 1)
     send(14).start()
@@ -174,6 +173,10 @@
         def _():
             pack_first(*pair_of(p + 1))
 
+        @pl.when(p == 6)
+        def _():
+            pack_first(0, 1)
+
         @pl.loop((n_dev * (p - 1)) // 6, (n_dev * p) // 6)
         def _(d):
             vbuf[d] = pack(d, start1, size1)
@@ -182,12 +185,11 @@
             def _():
                 keep(d - 1).start()
 
-    pack_first(0, 1)
-    keep(n_dev - 1).start()
-    route_gates(x_ref, wr_ref, ids_ref, slot_ref, cols_ref)
     send(1).start()
     own = pltpu.make_async_copy(sbuf.at[0], got_ref.at[me], own_sem)
     own.start()
+    route_gates(x_ref, wr_ref, ids_ref, slot_ref, cols_ref)
+    keep(n_dev - 1).start()
     for p in (5, 6):
         for k in pair_of(p):
             send(k).wait_send()
@@ -432,18 +434,22 @@
         ff = w1.shape[2]
         n_exp = n * local
         cap = 4 * tok // n
+        slots, counts = pl.pallas_call(
+            functools.partial(route_slots, local, cap, n_exp),
+            out_shape=(jax.ShapeDtypeStruct((8, tok), I32), jax.ShapeDtypeStruct((n_exp, 128), I32)),
+            compiler_params=_params(),
+            name="route",
+        )(ids.T)
         smem = pl.BlockSpec(memory_space=pltpu.SMEM)
         vmem = pl.BlockSpec(memory_space=pltpu.VMEM)
         hbm = pl.BlockSpec(memory_space=pl.ANY)
         ship = pl.pallas_call(
-            functools.partial(ship_kernel, cap, n, CHUNKS, local),
-            in_specs=[vmem, vmem, vmem],
+            functools.partial(ship_kernel, cap, n, CHUNKS),
+            in_specs=[vmem] * 5,
             out_specs=[hbm, hbm, hbm, vmem],
             out_shape=[jax.ShapeDtypeStruct((n, size, dim), BF16) for _, size in CHUNKS]
             + [jax.ShapeDtypeStruct((n, n_exp, 128), I32), jax.ShapeDtypeStruct((tok, 8), F32)],
             scratch_shapes=[
-                pltpu.VMEM((8, tok), I32),
-                pltpu.VMEM((n_exp, 128), I32),
                 pltpu.VMEM((n, CHUNKS[0][1], dim), BF16),
                 pltpu.VMEM((n, CHUNKS[1][1], dim), BF16),
                 pltpu.SemaphoreType.DMA((n,)),
@@ -460,7 +466,7 @@
             cost_estimate=pl.CostEstimate(flops=10**11, bytes_accessed=1, transcendentals=0),
             name="ship",
         )
-        first_rows, second_rows, every, cols = ship(ids.T, w_router.T, x)
+        first_rows, second_rows, every, cols = ship(slots, counts, ids.T, w_router.T, x)
         at = lax.axis_index("ep") * local
         per_exp = lax.dynamic_slice(every, (0, at, 0), (n, local, 1))[:, :, 0]
         ends = jnp.cumsum(per_exp, axis=1).T

time: 344 us -> 342 us (level)
  starting transfers between devices: 13.1 us -> 8.48 us
    all_to_all x1, starting transfers between devices: 9.64 us -> 5.02 us  [body(): got = lax.all_to_all(second_rows, 'ep', 0, 0, tiled=True)]
    pallas_call x1 -> x2, Pallas kernels: 79.5 us -> 81.3 us  [the longest x1 79.4 us: body(): ship(slots, counts, ids.T, w_router.T, x)]
where the time goes in v1:
time: 342 us; the launch traced here: 338 us
  Pallas kernels  324 us (95%)
  starting transfers between devices  8.48 us (2%)
  local copies, waits for them, and re-layouts  5.29 us (2%)
    pallas_call x2, Pallas kernels, body(): made = made(bounds, got.reshape(rows, dim), w1, w3, w2)  160 us
    pallas_call x1, Pallas kernels, body(): pl.pallas_call(functools.partial(bring_kernel, cap, n, CHUNKS), in_specs=...  82.7 us
    pallas_call x1, Pallas kernels, body(): ship(slots, counts, ids.T, w_router.T, x)  79.4 us
  transfers between devices with their start and end apart: 2, of which 0 were waited for; matrix products, arithmetic and copies ran while one was open for 0% of the time, Pallas kernels for 47%

profile of v1, /device:TPU:11, one launch (start us, length us, event | category | flops | bytes accessed | tf_op | source)
XLA Modules:
  0.0 338.2 jit_solution(2025149616618970390)
XLA Ops:
  0.0 1.9 route.1
  1.9 79.4 %ship.1 = (bf16[16,256,768]{2,1,0:T(8,128)(2,1)}, bf16[16,256,768]{2,1,0:T(8,128)(2,1)}, s32[16,32,128]{2,1,0:T(8,128)}, f32[2048,8]{1,0:T(8,128)}) custom-call(s32[8,2048]{1,0:T(8,128)} %get-tuple-element.11.slot_ref, s32[32,128]{1,0:T(8,128)} %get-tuple-element.12.cnt_ref, s32[2,2048]{1,0:T(2,128)} %bitcast.11, f32[32,768]{1,0:T(8,128)} %bitcast.14, ...), custom_call_target="tpu_custom_call" | custom-call | flops 99999997952 | bytes 1 | tf_op jit(solution)/shard_map/ship/pallas_call | solution.py:469
  81.3 5.0 %all-to-all-start = ((bf16[16,256,768]{2,1,0:T(8,128)(2,1)}), bf16[16,256,768]{2,1,0:T(8,128)(2,1)}, u32[]{:S(2)}, u32[]{:S(2)}) async-start(bf16[16,256,768]{2,1,0:T(8,128)(2,1)} %get-tuple-element.14), calls=%async_computation | async-start | bytes 12582912 | tf_op jit(solution)/shard_map/all_to_all | solution.py:478
  86.3 0.8 constant_dynamic-slice_fusion
  87.2 0.1 copy.7
  87.3 0.6 concatenate.3.bound_ref
  87.9 79.3 %shard_map.65 = bf16[4096,768]{1,0:T(8,128)(2,1)} custom-call(s32[3,16]{1,0:T(4,128)} %concatenate.3.bound_ref, bf16[4096,768]{1,0:T(8,128)(2,1)} %bitcast.15, bf16[2,768,3072]{2,1,0:T(8,128)(2,1)} %w1_hbm.3, bf16[2,768,3072]{2,1,0:T(8,128)(2,1)} %w3_hbm.3, bf16[2,3072,768]{2,1,0:T(8,128)(2,1)} %w2_hbm.3), custom_call_target="tpu_custom_call" | custom-call | flops 57982058496 | bytes 1 | tf_op jit(solution)/shard_map/pallas_call | solution.py:502
  167.2 0.0 all-to-all-done
  167.2 3.5 %all-to-all-start.1 = ((bf16[16,256,768]{2,1,0:T(8,128)(2,1)}), bf16[16,256,768]{2,1,0:T(8,128)(2,1)}, u32[]{:S(2)}, u32[]{:S(2)}) async-start(bf16[16,256,768]{2,1,0:T(8,128)(2,1)} %bitcast.9), calls=%async_computation.1 | async-start | bytes 12582912 | tf_op jit(solution)/shard_map/all_to_all | solution.py:504
  170.7 81.0 %shard_map.64 = bf16[4096,768]{1,0:T(8,128)(2,1)} custom-call(s32[3,16]{1,0:T(4,128)} %concatenate.3.bound_ref, bf16[4096,768]{1,0:T(8,128)(2,1)} %bitcast.4.x_hbm, bf16[2,768,3072]{2,1,0:T(8,128)(2,1)} %w1_hbm.3, bf16[2,768,3072]{2,1,0:T(8,128)(2,1)} %w3_hbm.3, bf16[2,3072,768]{2,1,0:T(8,128)(2,1)} %w2_hbm.3), custom_call_target="tpu_custom_call" | custom-call | flops 57982058496 | bytes 1 | tf_op jit(solution)/shard_map/pallas_call | solution.py:502
  251.7 0.0 all-to-all-done.1
  251.7 82.7 %bring.1 = bf16[2048,768]{1,0:T(8,128)(2,1)} custom-call(bf16[16,256,768]{2,1,0:T(8,128)(2,1)} %bitcast.16, bf16[4096,768]{1,0:T(8,128)(2,1)} %bitcast.8.back_hbm, f32[2048,8]{1,0:T(8,128)} %get-tuple-element.16.cols_ref), custom_call_target="tpu_custom_call" | custom-call | flops 99999997952 | bytes 1 | tf_op jit(solution)/shard_map/bring/pallas_call | solution.py:505
  334.4 3.8 %copy.9 = bf16[2048,768]{1,0:T(8,128)(2,1)} copy(bf16[2048,768]{1,0:T(8,128)(2,1)} %bring.1) | data formatting | bytes 6291456
  (1 shorter events, 0.0 us)
Async XLA Ops:
  81.3 85.9 %all-to-all-start = ((bf16[16,256,768]{2,1,0:T(8,128)(2,1)}), bf16[16,256,768]{2,1,0:T(8,128)(2,1)}, u32[]{:S(2)}, u32[]{:S(2)}) async-start(bf16[16,256,768]{2,1,0:T(8,128)(2,1)} %get-tuple-element.14), calls=%async_computation | async-start | bytes 12582912 | tf_op jit(solution)/shard_map/all_to_all | solution.py:478
  167.2 84.5 %all-to-all-start.1 = ((bf16[16,256,768]{2,1,0:T(8,128)(2,1)}), bf16[16,256,768]{2,1,0:T(8,128)(2,1)}, u32[]{:S(2)}, u32[]{:S(2)}) async-start(bf16[16,256,768]{2,1,0:T(8,128)(2,1)} %bitcast.9), calls=%async_computation.1 | async-start | bytes 12582912 | tf_op jit(solution)/shard_map/all_to_all | solution.py:504
